TPU v7x, 256 devices: a whole 4x4x8 slice. The times are simulated.
256 devices in a mesh: gx: 64 (over z_lo, x, y), gy: 4 (over z_hi, core).
Axes of the slice: x: 4, y: 4, z: 8 (z_hi: 2, z_lo: 4; z = z_hi * 4 + z_lo), core: 2. Of those that a mesh axis runs over, the one named last changes fastest.
Arguments:
- date_key: int32 [3145728], P(('gx', 'gy')), may hold values from 0 to 4095
- store_key: int32 [3145728], P(('gx', 'gy')), may hold values from 0 to 65535
- product_key: int32 [3145728], P(('gx', 'gy')), may hold values from 0 to 1048575
- revenue: bfloat16 [3145728], P(('gx', 'gy')), may hold values from -0.59765625 to 0.59765625
- row_counts: int32 [256], P(('gx', 'gy')), may hold values from 1 to 12288, 1966080 in all
- date_years: int32 [512], P('gx'), may hold values from -2147483648 to 2147483646
- date_flags: int32 [128], P('gx'), may hold values from -2147483648 to 2147483646
- store_flags: int32 [2048], P('gx'), may hold values from -2147483648 to 2147483646
- product_flags: int32 [32768], P('gx'), may hold values from -2147483648 to 2147483646
- brand_words: int32 [349696], P('gx'), may hold values from 0 to 1073741823
Outputs:
- revenue_groups: float32 [16, 1024], replicated
Inputs may be any that keep to these rules, and one draw needn't show every extreme that they name: Rows d * 12288 to d * 12288 + row_counts[d] - 1 of the fact arrays are live; the largest count equals 12288. `date_years`: date k's year code is in bits 4 * (k % 8) of word k // 8. `date_flags`: bit k % 32 of word k // 32 is the flag of row k. `store_flags`: bit k % 32 of word k // 32 is the flag of row k. `product_flags`: bit k % 32 of word k // 32 is the flag of row k. `brand_words`: product with shard o and local index l holds its brand code in bits 10 * (l % 3) of word o * 5464 + l // 3; words past a shard's products are unused.
All inputs are finite; a program needn't handle non-finite values. No bound on the sum of `row_counts` on one device may be relied on, other than what follows from the above.
Results may differ from a plain program's by a relative error of at most 0.0003.
Values sent between devices are 32-bit elements; how exact they have to be, the bound alone decides.
No kernel may reach another device: no remote copies, remote signals or barrier semaphores. Data moves between devices by JAX's collectives and lax.ppermute only.
A program may use at most 64 MiB of HBM per device.

v0:
```python
import jax
import jax.numpy as jnp
from jax import lax
from jax.sharding import PartitionSpec as P

BRANDS = 1024
YEARS = 16


def joined_along(blocks, dim):
    dims = list(blocks.shape[1:])
    dims[dim] *= blocks.shape[0]
    return jnp.moveaxis(blocks, 0, dim).reshape(dims)


def gather_together(arrays, axis, dims):
    flat = jnp.concatenate([a.reshape(-1) for a in arrays])
    lines, at, outs = (lax.all_gather(flat, axis), 0, [])
    for a, dim in zip(arrays, dims):
        blocks = lines[:, at : at + a.size].reshape(-1, *a.shape)
        outs.append(joined_along(blocks, dim))
        at += a.size
    return tuple(outs)


def from_everyone(value, axis):
    copies = jnp.broadcast_to(value, (lax.axis_size(axis), *value.shape))
    return lax.all_to_all(copies, axis, split_axis=0, concat_axis=0, tiled=True)


def collect(value, axis, dim):
    blocks = from_everyone(value, axis)
    return joined_along(blocks, dim)


def pick_bits(packed, position, width_bits):
    per_word = 32 // width_bits
    chosen = packed[position // per_word]
    shifted = jnp.right_shift(chosen, position % per_word * width_bits)
    return jnp.bitwise_and(shifted, (1 << width_bits) - 1)


def shards(
    date_key,
    store_key,
    product_key,
    revenue,
    row_counts,
    date_years,
    date_flags,
    store_flags,
    product_flags,
    brand_words,
):
    gx_count = lax.axis_size("gx")
    gy_count = lax.axis_size("gy")
    flag_shard = product_flags.shape[0]
    brand_shard = brand_words.shape[0]
    prod_shard = flag_shard * 32
    member = lax.axis_index("gy")
    brand_part = brand_shard // gy_count
    flag_part = flag_shard // gy_count
    brand_slice = lax.dynamic_slice_in_dim(brand_words, member * brand_part, brand_part, 0)
    flag_slice = lax.dynamic_slice_in_dim(product_flags, member * flag_part, flag_part, 0)
    year_words, date_bits, store_bits, flag_some, brand_some = gather_together(
        (date_years, date_flags, store_flags, flag_slice, brand_slice), "gx", (0, 0, 0, 0, 0)
    )
    product_bits, brand_table = (collect(flag_some, "gy", 0), collect(brand_some, "gy", 0))

    def brand_place(owner_idx, word_idx):
        return (
            word_idx // brand_part * (gx_count * brand_part)
            + owner_idx * brand_part
            + word_idx % brand_part
        )

    def flag_place(owner_idx, word_idx):
        return (
            word_idx // flag_part * (gx_count * flag_part)
            + owner_idx * flag_part
            + word_idx % flag_part
        )

    block_rows = min(4096, date_key.shape[0])
    row_count = row_counts[0]
    block_total = (row_count + block_rows - 1) // block_rows
    high_groups = YEARS * BRANDS // 128

    def add_block(block_idx, totals):
        first_row = block_idx * block_rows
        date_block = lax.dynamic_slice_in_dim(date_key, first_row, block_rows, 0)
        store_block = lax.dynamic_slice_in_dim(store_key, first_row, block_rows, 0)
        product_block = lax.dynamic_slice_in_dim(product_key, first_row, block_rows, 0)
        money_block = lax.dynamic_slice_in_dim(revenue, first_row, block_rows, 0)
        live_rows = first_row + lax.iota(jnp.int32, block_rows) < row_count
        year_code = pick_bits(year_words, date_block, 4)
        owner_idx = product_block // prod_shard
        local_idx = product_block % prod_shard
        flag_word = product_bits[flag_place(owner_idx, local_idx // 32)]
        product_pass = jnp.bitwise_and(jnp.right_shift(flag_word, local_idx % 32), 1)
        passed = (
            pick_bits(date_bits, date_block, 1)
            * pick_bits(store_bits, store_block, 1)
            * product_pass
        )
        word_val = brand_table[brand_place(owner_idx, local_idx // 3)]
        brand_code = jnp.bitwise_and(jnp.right_shift(word_val, local_idx % 3 * 10), 1023)
        kept_rows = live_rows & (passed == 1)
        amount = jnp.where(kept_rows, money_block, jnp.zeros_like(money_block))
        high_row = year_code * (BRANDS // 128) + brand_code // 128
        weighted = jnp.where(
            lax.iota(jnp.int32, high_groups)[:, None] == high_row[None, :],
            amount[None, :],
            jnp.zeros((), jnp.bfloat16),
        )
        low_hot = (lax.iota(jnp.int32, 128)[:, None] == (brand_code % 128)[None, :]).astype(
            jnp.bfloat16
        )
        return totals + lax.dot_general(
            weighted, low_hot, (((1,), (1,)), ((), ())), preferred_element_type=jnp.float32
        )

    totals = lax.fori_loop(0, block_total, add_block, jnp.zeros((high_groups, 128), jnp.float32))
    group_sums = totals.reshape(YEARS, BRANDS)
    result = lax.psum(group_sums, ("gx", "gy"))
    return result


def solution(mesh):
    placed = (
        P(("gx", "gy")),
        P(("gx", "gy")),
        P(("gx", "gy")),
        P(("gx", "gy")),
        P(("gx", "gy")),
        P("gx"),
        P("gx"),
        P("gx"),
        P("gx"),
        P("gx"),
    )
    return jax.shard_map(shards, mesh=mesh, in_specs=placed, out_specs=P(), check_vma=False)
```

profile of v0, /device:TPU:1, one launch (start us, length us, event | category | flops | bytes accessed | tf_op | source)
XLA Modules:
  0.0 855.9 jit_solution(2321840146524522188)
XLA Ops:
  6.5 0.8 dynamic_slice.34
  7.3 0.8 dynamic_slice.35
  8.1 0.8 concatenate.3
  8.8 163.3 %all-gather.1 = s32[64,1,1536]{2,1,0:T(1,128)S(1)} all-gather(s32[1,1,1536]{2,1,0:T(1,128)S(1)} %reshape.91), channel_id=2, replica_groups=mesh['gx'=64,'gy'=4] {'gx'}, dimensions={0}, use_global_device_ids=true | all-gather | bytes 399360 | tf_op jit(solution)/shard_map/all_gather | solution.py:18
  172.2 0.1 slice.31
  172.4 0.3 broadcast_in_dim.74
  172.7 1.8 broadcast_in_dim.75
  174.5 36.1 %all-to-all-start = ((s32[4,1,87424]{2,1,0:T(1,128)}), s32[4,1,87424]{2,1,0:T(1,128)S(1)}, u32[]{:S(2)}, u32[]{:S(2)}) async-start(s32[4,1,87424]{2,1,0:T(1,128)} %broadcast_in_dim.75), calls=%async_computation | async-start | bytes 2797568 | tf_op jit(solution)/shard_map/all_to_all | solution.py:28
  210.5 0.1 slice_bitcast_fusion
  210.6 21.0 %all-to-all-done = s32[4,1,87424]{2,1,0:T(1,128)S(1)} async-done(((s32[4,1,87424]{2,1,0:T(1,128)}), s32[4,1,87424]{2,1,0:T(1,128)S(1)}, u32[]{:S(2)}, u32[]{:S(2)}) %all-to-all-start) | async-done | bytes 1398816 | tf_op jit(solution)/shard_map/all_to_all | solution.py:28
  231.7 0.7 broadcast_in_dim.77
  232.4 4.3 all-to-all-start.1
  236.6 0.0 all-reduce.2.cloned.1.call-start
  237.3 0.1 slice.33
  237.4 0.1 slice.32
  237.5 0.1 reshape.42
  237.6 0.1 reshape.41
  237.7 0.1 reshape.39
  237.8 4.3 reduce
  242.1 0.0 copy-start
  242.1 0.0 copy-start.1
  242.1 0.0 copy-start.2
  242.1 0.6 reshape.40
  242.7 1.4 all-to-all-done.1
  244.1 0.0 copy-done
  244.1 0.0 copy-done.1
  244.1 0.0 copy-done.2
  244.2 122.1 %while.13 = (s32[]{:T(128)}, f32[128,128]{1,0:T(8,128)S(1)}, s32[]{:T(128)}, s32[12288]{0:T(1024)S(1)}, s32[512]{0:T(512)S(1)}, /*index=5*/s32[12288]{0:T(1024)S...) while((s32[]{:T(128)}, f32[128,128]{1,0:T(8,128)S(1)}, ...), condition=%wide.region_1.2_spmd, body=%wide.region_0.1_spmd.sunk | while | flops 136892416 | bytes 860395 | solution.py:123
  244.2 0.1 fusion.65
  244.2 23.0 %gather_fusion.2 = s32[4096]{0:T(1024)S(1)} fusion(s32[32768]{0:T(1024)S(1)} %get-tuple-element.431, s32[4096]{0:T(1024)S(1)} %get-tuple-element.382), kind=kCustom, calls=%fused_computation.4.clone.1 | custom fusion | bytes 49152 | tf_op jit(solution)/shard_map/while/body/gather | solution.py:99
  267.3 0.1 fusion.66
  267.4 23.0 %gather_fusion.1 = s32[4096]{0:T(1024)S(1)} fusion(s32[349696]{0:T(1024)S(1)} %get-tuple-element.426, s32[4096]{0:T(1024)S(1)} %fusion.66), kind=kCustom, calls=%fused_computation.1.clone.1 | custom fusion | bytes 49152 | tf_op jit(solution)/shard_map/while/body/gather | solution.py:106
  290.5 25.9 %gather_fusion = s32[4096]{0:T(1024)S(1)} fusion(s32[512]{0:T(512)S(1)} %get-tuple-element.424, s32[4096]{0:T(1024)S(1)} %fusion.64), kind=kCustom, calls=%fused_computation.clone.1 | custom fusion | bytes 49152 | tf_op jit(solution)/shard_map/while/body/gather | solution.py:38
  316.4 24.7 %gather_fusion.4 = s32[4096]{0:T(1024)S(1)} fusion(s32[128]{0:T(128)S(1)} %get-tuple-element.428, s32[4096]{0:T(1024)S(1)} %get-tuple-element.384), kind=kCustom, calls=%fused_computation.2.clone.1 | custom fusion | bytes 49152 | tf_op jit(solution)/shard_map/while/body/gather | solution.py:38
  341.1 0.1 fusion.67
  341.2 23.0 %gather_fusion.3 = s32[4096]{0:T(1024)S(1)} fusion(s32[2048]{0:T(1024)S(1)} %get-tuple-element.430, s32[4096]{0:T(1024)S(1)} %get-tuple-element.383), kind=kCustom, calls=%fused_computation.3.clone.1 | custom fusion | bytes 49152 | tf_op jit(solution)/shard_map/while/body/gather | solution.py:38
  364.2 1.4 fusion.68
  365.6 0.7 fusion.69
  366.3 0.6 reshape.44
  366.9 0.0 all-reduce.2.cloned.1.call-update
  366.9 480.6 %all-reduce.2.cloned.1.call-done = f32[16,1024]{1,0:T(8,128)} async-done(((f32[16,1024]{1,0:T(8,128)}), f32[16,1024]{1,0:T(8,128)}) %all-reduce.2.cloned.1.call-update) | async-done | bytes 65552 | tf_op jit(solution)/shard_map/psum | solution.py:125
  847.5 1.5 copy.22
  (6 shorter events, 0.1 us)
Async XLA Ops:
  174.5 57.2 %all-to-all-start = ((s32[4,1,87424]{2,1,0:T(1,128)}), s32[4,1,87424]{2,1,0:T(1,128)S(1)}, u32[]{:S(2)}, u32[]{:S(2)}) async-start(s32[4,1,87424]{2,1,0:T(1,128)} %broadcast_in_dim.75), calls=%async_computation | async-start | bytes 2797568 | tf_op jit(solution)/shard_map/all_to_all | solution.py:28
  232.4 11.7 %all-to-all-start.1 = ((s32[4,1,8192]{2,1,0:T(1,128)}), s32[4,1,8192]{2,1,0:T(1,128)S(1)}, u32[]{:S(2)}, u32[]{:S(2)}) async-start(s32[4,1,8192]{2,1,0:T(1,128)} %broadcast_in_dim.77), calls=%async_computation.1 | async-start | bytes 262144 | tf_op jit(solution)/shard_map/all_to_all | solution.py:28
  236.6 610.9 %all-reduce.2.cloned.1.call-start = ((), (), s32[]{:S(2)}) async-start(), calls=%async_computation.2 | async-start | bytes 131072 | tf_op jit(solution)/shard_map/psum | solution.py:125
  242.1 2.0 copy-start
  242.1 2.0 copy-start.1
  242.1 2.0 copy-start.2
Sparse Core Ops, SparseCore 0:
  367.0 480.4 all-reduce.1
where the time goes:
time: 856 us
  waiting for transfers between devices  503 us (59%)
  blocking collectives  163 us (19%)
  local copies, waits for them, and re-layouts  128 us (15%)
  starting transfers between devices  40.3 us (5%)
  between operations  14.2 us (2%)
    psum x1, waiting for transfers between devices, shards(): result = lax.psum(group_sums, ('gx', 'gy'))  481 us
    all_gather x1, blocking collectives, gather_together(): lines, at, outs = (lax.all_gather(flat, axis), 0, [])  163 us
    gather x3, local copies, waits for them, and re-layouts, pick_bits(): chosen = packed[position // per_word]  73.6 us
    all_to_all x2, starting transfers between devices, from_everyone(): return lax.all_to_all(copies, axis, split_axis=0, concat_axis=0, tiled=True)  40.3 us
    gather x1, local copies, waits for them, and re-layouts, add_block(): flag_word = product_bits[flag_place(owner_idx, local_idx // 32)]  23 us
    gather x1, local copies, waits for them, and re-layouts, add_block(): word_val = brand_table[brand_place(owner_idx, local_idx // 3)]  23 us
    all_to_all x2, waiting for transfers between devices, from_everyone(): return lax.all_to_all(copies, axis, split_axis=0, concat_axis=0, tiled=True)  22.5 us
  transfers between devices with their start and end apart: 3, of which 3 were waited for; matrix products, arithmetic and copies ran while one was open for 1% of the time, Pallas kernels for 0%

commit v1 on v0

--- a/solution.py
+++ b/solution.py
@@ -122,7 +122,8 @@
 
     totals = lax.fori_loop(0, block_total, add_block, jnp.zeros((high_groups, 128), jnp.float32))
     group_sums = totals.reshape(YEARS, BRANDS)
-    result = lax.psum(group_sums, ("gx", "gy"))
+    parts = lax.all_gather(group_sums, ("gx", "gy"))
+    result = jnp.sum(parts, axis=0)
     return result
 
 

time: 856 us -> 1050 us (1.23)
  waiting for transfers between devices: 503 us -> 690 us
    all_gather x0 -> x1, waiting for transfers between devices: none -> 667 us  [shards(): parts = lax.all_gather(group_sums, ('gx', 'gy'))]
    psum x1 -> x0, waiting for transfers between devices: 481 us -> none  [shards(): result = lax.psum(group_sums, ('gx', 'gy'))]
where the time goes in v1:
time: 1050 us
  waiting for transfers between devices  690 us (66%)
  blocking collectives  163 us (16%)
  local copies, waits for them, and re-layouts  127 us (12%)
  starting transfers between devices  40.3 us (4%)
  between operations  14.2 us (1%)
  other arithmetic  13.2 us (1%)
    all_gather x1, waiting for transfers between devices, shards(): parts = lax.all_gather(group_sums, ('gx', 'gy'))  667 us
    all_gather x1, blocking collectives, gather_together(): lines, at, outs = (lax.all_gather(flat, axis), 0, [])  163 us
    gather x3, local copies, waits for them, and re-layouts, pick_bits(): chosen = packed[position // per_word]  73.6 us
    all_to_all x2, starting transfers between devices, from_everyone(): return lax.all_to_all(copies, axis, split_axis=0, concat_axis=0, tiled=True)  40.3 us
    gather x1, local copies, waits for them, and re-layouts, add_block(): flag_word = product_bits[flag_place(owner_idx, local_idx // 32)]  23 us
    gather x1, local copies, waits for them, and re-layouts, add_block(): word_val = brand_table[brand_place(owner_idx, local_idx // 3)]  23 us
    all_to_all x2, waiting for transfers between devices, from_everyone(): return lax.all_to_all(copies, axis, split_axis=0, concat_axis=0, tiled=True)  22.5 us
  transfers between devices with their start and end apart: 3, of which 3 were waited for; matrix products, arithmetic and copies ran while one was open for 1% of the time, Pallas kernels for 0%

profile of v1, /device:TPU:1, one launch (start us, length us, event | category | flops | bytes accessed | tf_op | source)
XLA Modules:
  0.0 1048.5 jit_solution(2414784116842742830)
XLA Ops:
  6.5 0.8 dynamic_slice.34
  7.3 0.8 dynamic_slice.35
  8.1 0.8 concatenate.3
  8.8 163.3 %all-gather.1 = s32[64,1,1536]{2,1,0:T(1,128)S(1)} all-gather(s32[1,1,1536]{2,1,0:T(1,128)S(1)} %reshape.87), channel_id=2, replica_groups=mesh['gx'=64,'gy'=4] {'gx'}, dimensions={0}, use_global_device_ids=true | all-gather | bytes 399360 | tf_op jit(solution)/shard_map/all_gather | solution.py:18
  172.2 0.1 slice.31
  172.4 0.3 broadcast_in_dim.74
  172.7 1.8 broadcast_in_dim.75
  174.5 36.1 %all-to-all-start = ((s32[4,1,87424]{2,1,0:T(1,128)}), s32[4,1,87424]{2,1,0:T(1,128)S(1)}, u32[]{:S(2)}, u32[]{:S(2)}) async-start(s32[4,1,87424]{2,1,0:T(1,128)} %broadcast_in_dim.75), calls=%async_computation | async-start | bytes 2797568 | tf_op jit(solution)/shard_map/all_to_all | solution.py:28
  210.5 0.1 slice_bitcast_fusion
  210.6 21.0 %all-to-all-done = s32[4,1,87424]{2,1,0:T(1,128)S(1)} async-done(((s32[4,1,87424]{2,1,0:T(1,128)}), s32[4,1,87424]{2,1,0:T(1,128)S(1)}, u32[]{:S(2)}, u32[]{:S(2)}) %all-to-all-start) | async-done | bytes 1398816 | tf_op jit(solution)/shard_map/all_to_all | solution.py:28
  231.7 0.7 broadcast_in_dim.77
  232.4 4.3 all-to-all-start.1
  236.6 0.0 all-gather.4.cloned.1.call-start
  237.3 0.1 slice.33
  237.4 0.1 slice.32
  237.5 0.1 reshape.39
  237.6 0.1 reshape.38
  237.7 0.1 reshape.36
  237.8 4.3 reduce
  242.1 0.0 copy-start
  242.1 0.0 copy-start.1
  242.1 0.0 copy-start.2
  242.1 0.6 reshape.37
  242.7 1.4 all-to-all-done.1
  244.1 0.0 copy-done
  244.1 0.0 copy-done.1
  244.1 0.0 copy-done.2
  244.2 122.1 %while.13 = (s32[]{:T(128)}, f32[128,128]{1,0:T(8,128)S(1)}, s32[]{:T(128)}, s32[12288]{0:T(1024)S(1)}, s32[512]{0:T(512)S(1)}, /*index=5*/s32[12288]{0:T(1024)S...) while((s32[]{:T(128)}, f32[128,128]{1,0:T(8,128)S(1)}, ...), condition=%wide.region_1.2_spmd, body=%wide.region_0.1_spmd.sunk | while | flops 136892416 | bytes 860395 | solution.py:123
  244.2 0.1 fusion.65
  244.2 23.0 %gather_fusion.2 = s32[4096]{0:T(1024)S(1)} fusion(s32[32768]{0:T(1024)S(1)} %get-tuple-element.431, s32[4096]{0:T(1024)S(1)} %get-tuple-element.382), kind=kCustom, calls=%fused_computation.4.clone.1 | custom fusion | bytes 49152 | tf_op jit(solution)/shard_map/while/body/gather | solution.py:99
  267.3 0.1 fusion.66
  267.4 23.0 %gather_fusion.1 = s32[4096]{0:T(1024)S(1)} fusion(s32[349696]{0:T(1024)S(1)} %get-tuple-element.426, s32[4096]{0:T(1024)S(1)} %fusion.66), kind=kCustom, calls=%fused_computation.1.clone.1 | custom fusion | bytes 49152 | tf_op jit(solution)/shard_map/while/body/gather | solution.py:106
  290.5 25.9 %gather_fusion = s32[4096]{0:T(1024)S(1)} fusion(s32[512]{0:T(512)S(1)} %get-tuple-element.424, s32[4096]{0:T(1024)S(1)} %fusion.64), kind=kCustom, calls=%fused_computation.clone.1 | custom fusion | bytes 49152 | tf_op jit(solution)/shard_map/while/body/gather | solution.py:38
  316.4 24.7 %gather_fusion.4 = s32[4096]{0:T(1024)S(1)} fusion(s32[128]{0:T(128)S(1)} %get-tuple-element.428, s32[4096]{0:T(1024)S(1)} %get-tuple-element.384), kind=kCustom, calls=%fused_computation.2.clone.1 | custom fusion | bytes 49152 | tf_op jit(solution)/shard_map/while/body/gather | solution.py:38
  341.1 0.1 fusion.67
  341.2 23.0 %gather_fusion.3 = s32[4096]{0:T(1024)S(1)} fusion(s32[2048]{0:T(1024)S(1)} %get-tuple-element.430, s32[4096]{0:T(1024)S(1)} %get-tuple-element.383), kind=kCustom, calls=%fused_computation.3.clone.1 | custom fusion | bytes 49152 | tf_op jit(solution)/shard_map/while/body/gather | solution.py:38
  364.2 1.4 fusion.68
  365.6 0.7 fusion.69
  366.3 0.6 all_gather_reshape.3
  366.9 0.0 all-gather.4.cloned.1.call-update
  366.9 667.5 %all-gather.4.cloned.1.call-done = f32[256,16,1024]{2,1,0:T(8,128)} async-done(((f32[1,16,1024]{2,1,0:T(8,128)}), f32[256,16,1024]{2,1,0:T(8,128)}) %all-gather.4.cloned.1.call-update) | async-done | bytes 16777232 | tf_op jit(solution)/shard_map/all_gather | solution.py:125
  1034.4 7.3 reduce_sum.9
  (6 shorter events, 0.1 us)
Async XLA Ops:
  174.5 57.2 %all-to-all-start = ((s32[4,1,87424]{2,1,0:T(1,128)}), s32[4,1,87424]{2,1,0:T(1,128)S(1)}, u32[]{:S(2)}, u32[]{:S(2)}) async-start(s32[4,1,87424]{2,1,0:T(1,128)} %broadcast_in_dim.75), calls=%async_computation | async-start | bytes 2797568 | tf_op jit(solution)/shard_map/all_to_all | solution.py:28
  232.4 11.7 %all-to-all-start.1 = ((s32[4,1,8192]{2,1,0:T(1,128)}), s32[4,1,8192]{2,1,0:T(1,128)S(1)}, u32[]{:S(2)}, u32[]{:S(2)}) async-start(s32[4,1,8192]{2,1,0:T(1,128)} %broadcast_in_dim.77), calls=%async_computation.1 | async-start | bytes 262144 | tf_op jit(solution)/shard_map/all_to_all | solution.py:28
  236.6 797.7 %all-gather.4.cloned.1.call-start = ((), (), s32[]{:S(2)}) async-start(), calls=%async_computation.2 | async-start | bytes 16842752 | tf_op jit(solution)/shard_map/all_gather | solution.py:125
  242.1 2.0 copy-start
  242.1 2.0 copy-start.1
  242.1 2.0 copy-start.2
Sparse Core Ops, SparseCore 0:
  367.0 667.2 all-gather.3
